TPU v7x, 32 devices: a whole 2x2x4 slice. The times are simulated.
32 devices in a mesh: ea: 8 (over z, y), sa: 4 (over x, core).
Axes of the slice: x: 2, y: 2, z: 4, core: 2. Of those that a mesh axis runs over, the one named last changes fastest.
Arguments:
- lesser: bfloat16 [2, 1024, 2, 256, 256], P(None, 'ea', None, 'sa'), may hold values from -30 to 30, as said below
- greater: bfloat16 [2, 1024, 2, 256, 256], P(None, 'ea', None, 'sa'), may hold values from -30 to 30, as said below
Outputs:
- polar: float32 [2, 1024, 2, 256, 256], P(None, 'ea', None, 'sa')
- pol_norm: float32 [1], replicated
Inputs may be any that keep to these rules, and one draw needn't show every extreme that they name: `lesser`: Real-valued entries, independent from energy to energy. `greater`: Real-valued entries, independent from energy to energy.
All inputs are finite; a program needn't handle non-finite values.
Results may differ from a plain program's by a relative error of at most 0.0049.
Values may be sent and summed in bfloat16 or wider, within the bound.
A program may use at most 320 MiB of HBM per device.

v0:
```python
import math
import jax
import jax.numpy as jnp
from jax import lax
from jax.sharding import PartitionSpec as P

NE = 1024
ORB = 256
BLOCKS = 2


def energy_tables(count):
    index = jnp.arange(count, dtype=jnp.int32)
    phase = index[:, None] * index[None, :] % count
    angle = phase.astype(jnp.float32) * (2.0 * math.pi / count)
    return (jnp.cos(angle).astype(jnp.bfloat16), jnp.sin(angle).astype(jnp.bfloat16))


def spectra(columns, cosine, sine):
    stacked = jnp.concatenate(columns, axis=1)
    return (
        jnp.dot(cosine, stacked, preferred_element_type=jnp.float32),
        jnp.dot(sine, stacked, preferred_element_type=jnp.float32),
    )


def split_spectrum(cos_part, sin_part, which, width):
    real_cols = slice(2 * which * width, (2 * which + 1) * width)
    imag_cols = slice((2 * which + 1) * width, (2 * which + 2) * width)
    spec_re = cos_part[:, real_cols] + sin_part[:, imag_cols]
    spec_im = cos_part[:, imag_cols] - sin_part[:, real_cols]
    return (spec_re, spec_im)


def polarize(less_re, less_im, great_re, great_im, cosine, sine, count):
    width = less_re.shape[1]
    prod_re = (less_re * great_re + less_im * great_im).astype(jnp.bfloat16)
    prod_im = (less_im * great_re - less_re * great_im).astype(jnp.bfloat16)
    cos_part, sin_part = spectra([prod_re, prod_im], cosine, sine)
    corr_re = cos_part[:, :width] - sin_part[:, width:]
    corr_im = cos_part[:, width:] + sin_part[:, :width]
    weight = float(count) ** (-1.5)
    return jnp.stack([weight * corr_im, -weight * corr_re])


def both_spectra(less_pairs, great_pairs, cosine, sine):
    energies = less_pairs.shape[1]
    width = less_pairs[0].size // energies
    cos_part, sin_part = spectra(
        [
            less_pairs[0].reshape(energies, width),
            less_pairs[1].reshape(energies, width),
            great_pairs[0].reshape(energies, width),
            great_pairs[1].reshape(energies, width),
        ],
        cosine,
        sine,
    )
    less_re, less_im = split_spectrum(cos_part, sin_part, 0, width)
    great_re, great_im = split_spectrum(cos_part, sin_part, 1, width)
    return (less_re, less_im, great_re, great_im)


def body(lesser, greater):
    cosine, sine = energy_tables(NE)
    less_pairs, great_pairs = (
        lax.all_to_all(lesser, "ea", split_axis=4, concat_axis=1, tiled=True),
        lax.all_to_all(greater, "ea", split_axis=4, concat_axis=1, tiled=True),
    )
    shape = less_pairs.shape
    less_re, less_im, great_re, great_im = both_spectra(less_pairs, great_pairs, cosine, sine)
    polar_local = polarize(less_re, less_im, great_re, great_im, cosine, sine, NE).reshape(shape)
    total = jnp.sum(polar_local * polar_local)
    polar = lax.all_to_all(polar_local, "ea", split_axis=1, concat_axis=4, tiled=True)
    norm_total = lax.psum(total, ("ea", "sa"))
    pol_norm = jnp.sqrt(norm_total / (NE * BLOCKS * ORB * ORB) + 1e-06).reshape(1)
    return (polar, pol_norm)


def solution(mesh):
    return jax.shard_map(
        body,
        mesh=mesh,
        in_specs=(P(None, "ea", None, "sa", None), P(None, "ea", None, "sa", None)),
        out_specs=(P(None, "ea", None, "sa", None), P()),
        check_vma=False,
    )
```

profile of v0, /device:TPU:0, one launch (start us, length us, event | category | flops | bytes accessed | tf_op | source)
XLA Modules:
  0.0 2305.2 jit_solution(13442088749279677112)
XLA Ops:
  0.6 25.8 %copy.41 = bf16[2,128,2,64,256]{1,3,2,0,4:T(8,128)(2,1)} copy(bf16[2,128,2,64,256]{4,3,2,1,0:T(8,128)(2,1)} %param.2) | data formatting | bytes 33554432 | tf_op args[0]
  26.4 7.3 all-to-all-start
  33.7 25.9 %copy.45 = bf16[2,128,2,64,256]{1,3,2,0,4:T(8,128)(2,1)} copy(bf16[2,128,2,64,256]{4,3,2,1,0:T(8,128)(2,1)} %param.3) | data formatting | bytes 33554432 | tf_op args[1]
  59.7 337.0 %all-to-all-done = bf16[2,128,2,64,256]{1,3,2,0,4:T(8,128)(2,1)} async-done(((bf16[2,128,2,64,256]{1,3,2,0,4:T(8,128)(2,1)}), bf16[2,128,2,64,256]{1,3,2,0,4:T(8,128)(2,1)}, u32[]{:S(2)}, u32[]{:S(2)}) %all-to-all-start) | async-done | bytes 16777248 | tf_op jit(solution)/shard_map/all_to_all | solution.py:67
  396.7 5.7 all-to-all-start.1
  402.5 16.3 cosine_convert_fusion.9
  418.7 15.7 sine_convert_fusion.9
  434.4 16.3 cosine_convert_fusion.8
  450.7 16.4 sine_convert_fusion.8
  467.1 12.3 copy.42
  479.4 7.0 fusion.31
  486.4 15.1 copy.43
  501.5 15.5 copy.44
  517.0 9.4 bitcast_dynamic-update-slice_fusion.3
  526.4 238.1 %all-to-all-done.1 = bf16[2,128,2,64,256]{1,3,2,0,4:T(8,128)(2,1)} async-done(((bf16[2,128,2,64,256]{1,3,2,0,4:T(8,128)(2,1)}), bf16[2,128,2,64,256]{1,3,2,0,4:T(8,128)(2,1)}, u32[]{:S(2)}, u32[]{:S(2)}) %all-to-all-start.1) | async-done | bytes 16777248 | tf_op jit(solution)/shard_map/all_to_all | solution.py:68
  764.5 12.3 copy.46
  776.8 6.9 fusion.30
  783.7 15.1 copy.47
  798.8 15.3 copy.48
  814.1 9.4 bitcast_dynamic-update-slice_fusion.2
  823.5 9.4 bitcast_dynamic-update-slice_fusion.1
  832.9 9.8 bitcast_dynamic-update-slice_fusion
  842.7 45.0 %fusion.10 = f32[1024,16384]{1,0:T(8,128)} fusion(bf16[1024,16384]{0,1:T(8,128)(2,1)} %bitcast_dynamic-update-slice_fusion, bf16[1024,1024]{1,0:T(8,128)(2,1)} %cosine_convert_fusion.9), kind=kOutput, calls=%fused_computation.30 | convolution fusion | flops 34359738368 | bytes 102760448 | tf_op jit(solution)/shard_map/dot_general | solution.py:22
  887.7 44.3 %fusion.11 = f32[1024,16384]{1,0:T(8,128)} fusion(bf16[1024,16384]{0,1:T(8,128)(2,1)} %bitcast_dynamic-update-slice_fusion, bf16[1024,1024]{1,0:T(8,128)(2,1)S(1)} %sine_convert_fusion.9), kind=kOutput, calls=%fused_computation.31 | convolution fusion | flops 34359738368 | bytes 102760448 | tf_op jit(solution)/shard_map/dot_general | solution.py:23
  931.9 49.1 %add_convert_fusion = (bf16[1024,4096]{1,0:T(8,128)(2,1)}, bf16[1024,4096]{1,0:T(8,128)(2,1)}) fusion(f32[1024,16384]{1,0:T(8,128)} %fusion.11, f32[1024,16384]{1,0:T(8,128)} %fusion.10), kind=kLoop, calls=%fused_computation.12 | loop fusion | flops 50331648 | bytes 150994944 | tf_op jit(solution)/shard_map/convert_element_type | solution.py:37
  981.0 0.0 copy-start
  981.0 26.1 %fusion.3 = f32[1024,8192]{1,0:T(8,128)} fusion(bf16[1024,4096]{1,0:T(8,128)(2,1)} %get-tuple-element.11, bf16[1024,4096]{1,0:T(8,128)(2,1)} %get-tuple-element.10, bf16[1024,1024]{1,0:T(8,128)(2,1)} %cosine_convert_fusion.8), kind=kOutput, calls=%fused_computation.14 | convolution fusion | flops 17213423616 | bytes 52428800 | tf_op jit(solution)/shard_map/dot_general | solution.py:22
  1007.1 0.0 copy-done
  1007.1 25.7 %fusion.2 = f32[1024,8192]{1,0:T(8,128)} fusion(bf16[1024,4096]{1,0:T(8,128)(2,1)} %get-tuple-element.11, bf16[1024,4096]{1,0:T(8,128)(2,1)} %get-tuple-element.10, bf16[1024,1024]{1,0:T(8,128)(2,1)S(1)} %copy-done), kind=kOutput, calls=%fused_computation.13 | convolution fusion | flops 17213423616 | bytes 52428800 | tf_op jit(solution)/shard_map/dot_general | solution.py:23
  1032.9 34.7 %fusion.1 = (f32[1024,4096]{1,0:T(8,128)}, f32[1024,4096]{1,0:T(8,128)}) fusion(f32[1024,8192]{1,0:T(8,128)} %fusion.2, f32[1024,8192]{1,0:T(8,128)} %fusion.3), kind=kLoop, calls=%fused_computation.5 | loop fusion | flops 16777216 | bytes 100663296 | tf_op jit(solution)/shard_map/mul | solution.py:43
  1067.5 17.4 copy.49
  1085.0 17.5 copy.50
  1102.5 26.3 %multiply_reduce_fusion = (f32[]{:T(128)}, f32[2,1024,2,64,32]{1,4,3,2,0:T(8,128)}) fusion(f32[1,1024,2,64,32]{1,4,3,2,0:T(8,128)} %bitcast.50, f32[1,1024,2,64,32]{1,4,3,2,0:T(8,128)} %bitcast.49), kind=kLoop, calls=%fused_computation.1 | loop fusion | flops 25165824 | bytes 67108864 | tf_op jit(solution)/shard_map/reduce_sum | solution.py:73
  1128.7 59.1 %copy.51 = f32[2,1024,2,64,32]{3,4,2,0,1:T(8,128)} copy(f32[2,1024,2,64,32]{1,4,3,2,0:T(8,128)} %get-tuple-element.15) | data formatting | bytes 67108864 | tf_op jit(solution)/shard_map/stack | solution.py:43
  1187.8 84.9 %reshape.21 = f32[8,1,1048576]{2,1,0:T(1,128)} reshape(f32[1024,2,2,32,64]{4,3,2,1,0:T(8,128)} %bitcast.38) | data formatting | bytes 67108864
  1272.8 7.1 all-to-all-start.2
  1279.8 741.6 %psum.7 = f32[]{:T(128)} all-reduce(f32[]{:T(128)} %get-tuple-element.14), channel_id=1, replica_groups=mesh['ea'=8,'sa'=4] {'ea','sa'}, use_global_device_ids=true, to_apply=%region_1.2 | all-reduce | flops 1 | bytes 8 | tf_op jit(solution)/shard_map/psum | solution.py:75
  2022.2 0.0 all-to-all-done.2
  2022.2 0.5 broadcast.30
  2022.7 98.8 %reduce = f32[8,1048576]{1,0:T(8,128)} reduce(f32[8,1,1048576]{2,1,0:T(1,128)} %all-to-all-done.2, f32[]{:T(128)} %broadcast.30), dimensions={1}, to_apply=%all_to_all.41.reduce_sub_computation | reduce | bytes 67108864 | tf_op jit(solution)/shard_map/all_to_all | solution.py:74
  2121.5 91.3 %reshape.22 = f32[1024,2,2,32,64]{4,3,2,1,0:T(8,128)} reshape(f32[8,1048576]{1,0:T(8,128)} %reduce) | data formatting | bytes 67108864
  2212.8 56.9 %copy.53 = f32[2,128,2,64,8,32]{1,5,4,3,2,0:T(8,128)} copy(f32[2,128,2,64,8,32]{3,5,2,0,1,4:T(8,128)} %bitcast.10) | data formatting | bytes 67108864 | tf_op jit(solution)/shard_map/all_to_all | solution.py:74
  2269.8 33.8 %copy.54 = f32[2,128,2,64,256]{4,3,2,1,0:T(8,128)} copy(f32[2,128,2,64,256]{1,4,3,2,0:T(8,128)} %bitcast.48) | data formatting | bytes 67108864
Async XLA Ops:
  26.4 370.3 %all-to-all-start = ((bf16[2,128,2,64,256]{1,3,2,0,4:T(8,128)(2,1)}), bf16[2,128,2,64,256]{1,3,2,0,4:T(8,128)(2,1)}, u32[]{:S(2)}, u32[]{:S(2)}) async-start(bf16[2,128,2,64,256]{1,3,2,0,4:T(8,128)(2,1)} %copy.41), calls=%async_computation | async-start | bytes 33554432 | tf_op jit(solution)/shard_map/all_to_all | solution.py:67
  396.7 367.8 %all-to-all-start.1 = ((bf16[2,128,2,64,256]{1,3,2,0,4:T(8,128)(2,1)}), bf16[2,128,2,64,256]{1,3,2,0,4:T(8,128)(2,1)}, u32[]{:S(2)}, u32[]{:S(2)}) async-start(bf16[2,128,2,64,256]{1,3,2,0,4:T(8,128)(2,1)} %copy.45), calls=%async_computation.1 | async-start | bytes 33554432 | tf_op jit(solution)/shard_map/all_to_all | solution.py:68
  981.0 26.1 %copy-start = (bf16[1024,1024]{1,0:T(8,128)(2,1)S(1)}, bf16[1024,1024]{1,0:T(8,128)(2,1)}, u32[]{:S(2)}) copy-start(bf16[1024,1024]{1,0:T(8,128)(2,1)} %sine_convert_fusion.8) | copy-start | bytes 6291460
  1272.8 749.4 %all-to-all-start.2 = ((f32[8,1,1048576]{2,1,0:T(1,128)}), f32[8,1,1048576]{2,1,0:T(1,128)}, u32[]{:S(2)}, u32[]{:S(2)}) async-start(f32[8,1,1048576]{2,1,0:T(1,128)} %reshape.21), calls=%async_computation.2 | async-start | bytes 67108864 | tf_op jit(solution)/shard_map/all_to_all | solution.py:74
where the time goes:
time: 2320 us; the launch traced here: 2310 us
  blocking collectives  742 us (32%)
  waiting for transfers between devices  575 us (25%)
  local copies, waits for them, and re-layouts  551 us (24%)
  other arithmetic  273 us (12%)
  matrix products  141 us (6%)
    psum x1, blocking collectives, body(): norm_total = lax.psum(total, ('ea', 'sa'))  742 us
    all_to_all x1, waiting for transfers between devices, body(): lax.all_to_all(lesser, 'ea', split_axis=4, concat_axis=1, tiled=True)  337 us
    unnamed x10, local copies, waits for them, and re-layouts  290 us
    all_to_all x1, waiting for transfers between devices, body(): lax.all_to_all(greater, 'ea', split_axis=4, concat_axis=1, tiled=True)  238 us
    all_to_all x1, other arithmetic, body(): lax.all_to_all(polar_local, 'ea', split_axis=1, concat_axis=4, tiled=True)  98.8 us
    dot_general x2, matrix products, spectra(): jnp.dot(cosine, stacked, preferred_element_type=jnp.float32)  71.1 us
    dot_general x2, matrix products, spectra(): jnp.dot(sine, stacked, preferred_element_type=jnp.float32)  70 us
    another operation x1, local copies, waits for them, and re-layouts, polarize(): return jnp.stack([weight * corr_im, -weight * corr_re])  59.1 us
  transfers between devices with their start and end apart: 3, of which 2 were waited for; matrix products, arithmetic and copies ran while one was open for 6% of the time, Pallas kernels for 0%

commit v1 on v0

--- a/solution.py
+++ b/solution.py
@@ -71,7 +71,10 @@
     less_re, less_im, great_re, great_im = both_spectra(less_pairs, great_pairs, cosine, sine)
     polar_local = polarize(less_re, less_im, great_re, great_im, cosine, sine, NE).reshape(shape)
     total = jnp.sum(polar_local * polar_local)
-    polar = lax.all_to_all(polar_local, "ea", split_axis=1, concat_axis=4, tiled=True)
+    polar = jnp.concatenate(
+        lax.all_to_all(jnp.stack(jnp.split(polar_local, lax.axis_size("ea"), 1), 0), "ea", 0, 0),
+        axis=4,
+    )
     norm_total = lax.psum(total, ("ea", "sa"))
     pol_norm = jnp.sqrt(norm_total / (NE * BLOCKS * ORB * ORB) + 1e-06).reshape(1)
     return (polar, pol_norm)

time: 2320 us -> 1950 us (0.84)
  local copies, waits for them, and re-layouts: 551 us -> 290 us
  other arithmetic: 273 us -> 187 us
    unnamed x10 -> x12, local copies, waits for them, and re-layouts: 290 us -> 122 us
    all_to_all x1 -> x0, other arithmetic: 98.8 us -> none  [body(): lax.all_to_all(polar_local, 'ea', split_axis=1, concat_axis=4, tiled=True)]
    another operation x1 -> x0, local copies, waits for them, and re-layouts: 59.1 us -> none  [polarize(): return jnp.stack([weight * corr_im, -weight * corr_re])]
    all_to_all x2 -> x0, local copies, waits for them, and re-layouts: 57.5 us -> none  [body(): lax.all_to_all(polar_local, 'ea', split_axis=1, concat_axis=4, tiled=True)]
    reshape x0 -> x1, local copies, waits for them, and re-layouts: none -> 23.6 us  [body(): jnp.concatenate(lax.all_to_all(jnp.stack(jnp.split(polar_local, lax.axis_...]
  transfers between devices with their start and end apart: 3 -> 3, of which waited for: 2 -> 2; matrix products, arithmetic and copies ran while one was open for 6% -> 9% of each run, Pallas kernels for 0% -> 0%
where the time goes in v1:
time: 1950 us; the launch traced here: 1940 us
  blocking collectives  726 us (37%)
  waiting for transfers between devices  575 us (29%)
  local copies, waits for them, and re-layouts  290 us (15%)
  other arithmetic  187 us (10%)
  matrix products  141 us (7%)
  starting transfers between devices  20.4 us (1%)
    psum x1, blocking collectives, body(): norm_total = lax.psum(total, ('ea', 'sa'))  726 us
    all_to_all x1, waiting for transfers between devices, body(): lax.all_to_all(lesser, 'ea', split_axis=4, concat_axis=1, tiled=True)  337 us
    all_to_all x1, waiting for transfers between devices, body(): lax.all_to_all(greater, 'ea', split_axis=4, concat_axis=1, tiled=True)  238 us
    unnamed x12, local copies, waits for them, and re-layouts  122 us
    dot_general x2, matrix products, spectra(): jnp.dot(cosine, stacked, preferred_element_type=jnp.float32)  71 us
    dot_general x2, matrix products, spectra(): jnp.dot(sine, stacked, preferred_element_type=jnp.float32)  69.9 us
    convert_element_type x1, other arithmetic, polarize(): prod_re = (less_re * great_re + less_im * great_im).astype(jnp.bfloat16)  49.3 us
  transfers between devices with their start and end apart: 3, of which 2 were waited for; matrix products, arithmetic and copies ran while one was open for 9% of the time, Pallas kernels for 0%

profile of v1, /device:TPU:0, one launch (start us, length us, event | category | flops | bytes accessed | tf_op | source)
XLA Modules:
  0.0 1942.7 jit_solution(9563622262076796038)
XLA Ops:
  0.6 25.8 %copy.15 = bf16[2,128,2,64,256]{1,3,2,0,4:T(8,128)(2,1)} copy(bf16[2,128,2,64,256]{4,3,2,1,0:T(8,128)(2,1)} %param.2) | data formatting | bytes 33554432 | tf_op args[0]
  26.4 7.3 all-to-all-start
  33.7 25.9 %copy.19 = bf16[2,128,2,64,256]{1,3,2,0,4:T(8,128)(2,1)} copy(bf16[2,128,2,64,256]{4,3,2,1,0:T(8,128)(2,1)} %param.3) | data formatting | bytes 33554432 | tf_op args[1]
  59.7 337.0 %all-to-all-done = bf16[2,128,2,64,256]{1,3,2,0,4:T(8,128)(2,1)} async-done(((bf16[2,128,2,64,256]{1,3,2,0,4:T(8,128)(2,1)}), bf16[2,128,2,64,256]{1,3,2,0,4:T(8,128)(2,1)}, u32[]{:S(2)}, u32[]{:S(2)}) %all-to-all-start) | async-done | bytes 16777248 | tf_op jit(solution)/shard_map/all_to_all | solution.py:67
  396.7 5.8 all-to-all-start.1
  402.5 16.3 cosine_convert_fusion.9
  418.7 15.7 sine_convert_fusion.9
  434.4 16.2 cosine_convert_fusion.8
  450.7 16.4 sine_convert_fusion.8
  467.0 12.3 copy.16
  479.4 7.0 fusion.57
  486.4 15.1 copy.17
  501.5 15.3 copy.18
  516.7 9.4 bitcast_dynamic-update-slice_fusion.3
  526.2 238.4 %all-to-all-done.1 = bf16[2,128,2,64,256]{1,3,2,0,4:T(8,128)(2,1)} async-done(((bf16[2,128,2,64,256]{1,3,2,0,4:T(8,128)(2,1)}), bf16[2,128,2,64,256]{1,3,2,0,4:T(8,128)(2,1)}, u32[]{:S(2)}, u32[]{:S(2)}) %all-to-all-start.1) | async-done | bytes 16777248 | tf_op jit(solution)/shard_map/all_to_all | solution.py:68
  764.5 12.3 copy.20
  776.8 7.2 fusion.56
  784.0 15.1 copy.21
  799.1 15.3 copy.22
  814.4 9.4 bitcast_dynamic-update-slice_fusion.2
  823.8 9.4 bitcast_dynamic-update-slice_fusion.1
  833.2 9.6 bitcast_dynamic-update-slice_fusion
  842.8 44.9 %fusion.36 = f32[1024,16384]{1,0:T(8,128)} fusion(bf16[1024,16384]{0,1:T(8,128)(2,1)} %bitcast_dynamic-update-slice_fusion, bf16[1024,1024]{1,0:T(8,128)(2,1)} %cosine_convert_fusion.9), kind=kOutput, calls=%fused_computation.71 | convolution fusion | flops 34359738368 | bytes 102760448 | tf_op jit(solution)/shard_map/dot_general | solution.py:22
  887.7 44.2 %fusion.37 = f32[1024,16384]{1,0:T(8,128)} fusion(bf16[1024,16384]{0,1:T(8,128)(2,1)} %bitcast_dynamic-update-slice_fusion, bf16[1024,1024]{1,0:T(8,128)(2,1)S(1)} %sine_convert_fusion.9), kind=kOutput, calls=%fused_computation.72 | convolution fusion | flops 34359738368 | bytes 102760448 | tf_op jit(solution)/shard_map/dot_general | solution.py:23
  931.9 49.3 %add_convert_fusion = (bf16[1024,4096]{1,0:T(8,128)(2,1)}, bf16[1024,4096]{1,0:T(8,128)(2,1)}) fusion(f32[1024,16384]{1,0:T(8,128)} %fusion.37, f32[1024,16384]{1,0:T(8,128)} %fusion.36), kind=kLoop, calls=%fused_computation.29 | loop fusion | flops 50331648 | bytes 150994944 | tf_op jit(solution)/shard_map/convert_element_type | solution.py:37
  981.2 0.0 copy-start.2
  981.2 26.1 %fusion.5 = f32[1024,8192]{1,0:T(8,128)} fusion(bf16[1024,4096]{1,0:T(8,128)(2,1)} %get-tuple-element.7, bf16[1024,4096]{1,0:T(8,128)(2,1)} %get-tuple-element.6, bf16[1024,1024]{1,0:T(8,128)(2,1)} %cosine_convert_fusion.8), kind=kOutput, calls=%fused_computation.31 | convolution fusion | flops 17213423616 | bytes 52428800 | tf_op jit(solution)/shard_map/dot_general | solution.py:22
  1007.3 0.0 copy-done.2
  1007.3 25.7 %fusion.4 = f32[1024,8192]{1,0:T(8,128)} fusion(bf16[1024,4096]{1,0:T(8,128)(2,1)} %get-tuple-element.7, bf16[1024,4096]{1,0:T(8,128)(2,1)} %get-tuple-element.6, bf16[1024,1024]{1,0:T(8,128)(2,1)S(1)} %copy-done.2), kind=kOutput, calls=%fused_computation.30 | convolution fusion | flops 17213423616 | bytes 52428800 | tf_op jit(solution)/shard_map/dot_general | solution.py:23
  1033.0 34.7 %fusion.2 = (f32[1024,4096]{1,0:T(8,128)}, f32[1024,4096]{1,0:T(8,128)}) fusion(f32[1024,8192]{1,0:T(8,128)} %fusion.4, f32[1024,8192]{1,0:T(8,128)} %fusion.5), kind=kLoop, calls=%fused_computation.20 | loop fusion | flops 16777216 | bytes 100663296 | tf_op jit(solution)/shard_map/mul | solution.py:43
  1067.7 17.4 copy.23
  1085.1 17.4 copy.24
  1102.6 0.0 copy-start
  1102.6 0.0 copy-start.1
  1102.6 5.0 fusion.11
  1107.6 3.6 copy-done
  1111.2 4.8 copy-done.1
  1115.9 2.6 fusion.14
  1118.5 2.6 fusion.17
  1121.2 2.6 fusion.20
  1123.8 2.6 fusion.23
  1126.4 2.6 fusion.26
  1129.0 2.6 fusion.29
  1131.6 2.6 fusion.32
  1134.3 7.3 all-to-all-start.2
  1141.6 15.6 fusion.1
  1157.2 726.0 %psum.7 = f32[]{:T(128)} all-reduce(f32[]{:T(128)} %fusion.1), channel_id=1, replica_groups=mesh['ea'=8,'sa'=4] {'ea','sa'}, use_global_device_ids=true, to_apply=%region_1.2 | all-reduce | flops 1 | bytes 8 | tf_op jit(solution)/shard_map/psum | solution.py:78
  1883.9 0.0 all-to-all-done.2
  1883.9 23.6 %copy.25 = f32[2,128,2,64,8,32]{1,5,4,3,2,0:T(8,128)} copy(f32[2,128,2,64,8,32]{1,5,3,2,0,4:T(8,128)} %bitcast.16) | data formatting | bytes 67108864 | tf_op jit(solution)/shard_map/reshape | solution.py:74
  1907.5 33.8 %copy.26 = f32[2,128,2,64,256]{4,3,2,1,0:T(8,128)} copy(f32[2,128,2,64,256]{1,4,3,2,0:T(8,128)} %bitcast.93) | data formatting | bytes 67108864
Async XLA Ops:
  26.4 370.3 %all-to-all-start = ((bf16[2,128,2,64,256]{1,3,2,0,4:T(8,128)(2,1)}), bf16[2,128,2,64,256]{1,3,2,0,4:T(8,128)(2,1)}, u32[]{:S(2)}, u32[]{:S(2)}) async-start(bf16[2,128,2,64,256]{1,3,2,0,4:T(8,128)(2,1)} %copy.15), calls=%async_computation | async-start | bytes 33554432 | tf_op jit(solution)/shard_map/all_to_all | solution.py:67
  396.7 367.8 %all-to-all-start.1 = ((bf16[2,128,2,64,256]{1,3,2,0,4:T(8,128)(2,1)}), bf16[2,128,2,64,256]{1,3,2,0,4:T(8,128)(2,1)}, u32[]{:S(2)}, u32[]{:S(2)}) async-start(bf16[2,128,2,64,256]{1,3,2,0,4:T(8,128)(2,1)} %copy.19), calls=%async_computation.1 | async-start | bytes 33554432 | tf_op jit(solution)/shard_map/all_to_all | solution.py:68
  981.2 26.1 %copy-start.2 = (bf16[1024,1024]{1,0:T(8,128)(2,1)S(1)}, bf16[1024,1024]{1,0:T(8,128)(2,1)}, u32[]{:S(2)}) copy-start(bf16[1024,1024]{1,0:T(8,128)(2,1)} %sine_convert_fusion.8) | copy-start | bytes 6291460
  1102.6 8.6 copy-start
  1102.6 13.3 copy-start.1
  1134.3 749.7 %all-to-all-start.2 = ((f32[8,2,128,2,64,32]{2,5,4,3,1,0:T(8,128)}), f32[8,2,128,2,64,32]{2,5,4,3,1,0:T(8,128)}, u32[]{:S(2)}, u32[]{:S(2)}) async-start(f32[8,2,128,2,64,32]{2,5,4,3,1,0:T(8,128)} %fusion.32), calls=%async_computation.2 | async-start | bytes 67108864 | tf_op jit(solution)/shard_map/all_to_all | solution.py:75
